TPU v7x, 256 devices: a 4x2x16 block of a 4x16x16 slice. The times are simulated.
256 devices in a mesh: groups: 2 (over y), mp: 16 (over z), expert: 4 (over x), dp: 2 (over core).
Axes of the slice: x: 4, y: 2, z: 16, core: 2. Of those that a mesh axis runs over, the one named last changes fastest.
The devices are a block of a 4x16x16 slice.
Arguments:
- hidden_in: bfloat16 [1024, 4096], P(('groups', 'expert', 'dp'), 'mp'), parts along dimension 0, may hold values from -6 to 6
- norm_gain: bfloat16 [2, 4096], P(None, 'mp'), may hold values from 0.25 to 1.75
- expert_ids: int32 [2, 1024, 2], P(None, ('groups', 'expert', 'dp')), parts along dimension 1, may hold values from 0 to 3, all different within a row; in each aligned block of 64 rows (0 to 63, 64 to 127, ..., all dimensions but the last counted through in order) at most 64 rows name the same one
- gate_counts: int32 [2, 1024, 2], P(None, ('groups', 'expert', 'dp')), parts along dimension 1, may hold values from 8 to 15
- exit_layer: int32 [1024], P(('groups', 'expert', 'dp')), parts along dimension 0, may hold values from 1 to 2
- w_gate: bfloat16 [2, 4, 7168, 4096], P(None, 'expert', ('mp', 'dp')), may hold values from -0.09375 to 0.09375
- w_up: bfloat16 [2, 4, 7168, 4096], P(None, 'expert', ('mp', 'dp')), may hold values from -0.09375 to 0.09375
- w_down: bfloat16 [2, 4, 7168, 4096], P(None, 'expert', ('mp', 'dp')), may hold values from -0.0625 to 0.0625
Outputs:
- hidden_out: bfloat16 [1024, 4096], P(('groups', 'expert', 'dp'), 'mp'), parts along dimension 0
There are 2 independent parts, one for each index of `groups`. A program takes and returns all parts, laid end to end along the dimension named above; an argument that names none is the same for every part. Nothing has to cross between parts.
Inputs may be any that keep to these rules, and one draw needn't show every extreme that they name: `expert_ids`: A token's two ids in a layer differ. In the rows of one device in one layer (aligned blocks of 64 rows, layer by layer) some expert may be named by all 64 rows.
All inputs are finite; a program needn't handle non-finite values.
Results may differ from a plain program's by a relative error of at most 0.014.
Values may be sent and summed in bfloat16 or wider, within the bound.
A program may use at most 128 MiB of HBM per device.

v0:
```python
import jax
import jax.numpy as jnp
from jax import lax
from jax.sharding import PartitionSpec as P

LAYERS = 2
norm_floor = 0.1


def rows_first(arrays, axis, dims):
    turned = [jnp.moveaxis(a, dim, 0) for a, dim in zip(arrays, dims)]
    both = jnp.concatenate([t.reshape(len(t), -1) for t in turned], axis=1)
    whole, at, outs = (lax.all_gather(both, axis, axis=0, tiled=True), 0, [])
    for t, dim in zip(turned, dims):
        section = whole[:, at : at + t[0].size].reshape(-1, *t.shape[1:])
        outs.append(jnp.moveaxis(section, 0, dim))
        at += t[0].size
    return tuple(outs)


def side_by_side(arrays, axis, dim, along):
    ends, at = ([], 0)
    for a in arrays[:-1]:
        at += a.shape[along]
        ends.append(at)
    both = jnp.concatenate(arrays, axis=along)
    return tuple(jnp.split(lax.all_gather(both, axis, axis=dim, tiled=True), ends, axis=along))


def body(hidden_in, norm_gain, expert_ids, gate_counts, exit_layer, w_gate, w_up, w_down):
    experts = lax.axis_size("expert")
    shards = lax.axis_size("mp")
    tok_rows, slice_width = hidden_in.shape
    full_width = slice_width * shards
    contract = (((1,), (1,)), ((), ()))
    expert_range = jnp.arange(experts, dtype=jnp.int32)
    slot_range = jnp.arange(tok_rows, dtype=jnp.int32)
    current = hidden_in
    for layer_idx in range(LAYERS):
        counts = gate_counts[layer_idx].astype(jnp.float32)
        gate_share = counts / jnp.sum(counts, axis=1, keepdims=True)
        active = exit_layer > layer_idx
        matched = (expert_ids[layer_idx][:, :, None] == expert_range[None, None, :]) & active[
            :, None, None
        ]
        chosen = jnp.sum(matched.astype(jnp.int32), axis=1)
        weight_te = jnp.sum(jnp.where(matched, gate_share[:, :, None], jnp.float32(0.0)), axis=1)
        slot_rank = jnp.cumsum(chosen, axis=0) - chosen
        place_mask = (slot_rank.T[:, None, :] == slot_range[None, :, None]) & (
            chosen.T[:, None, :] > 0
        )
        place_bf = place_mask.astype(jnp.bfloat16)
        current_f32 = current.astype(jnp.float32)
        whole_rows, whole_gain = rows_first((current, norm_gain[layer_idx]), "mp", (1, 0))
        whole_f32 = whole_rows.astype(jnp.float32)
        sum_squares = jnp.sum(whole_f32 * whole_f32, axis=1)
        inv_rms = lax.rsqrt(sum_squares / full_width + norm_floor)
        normed = (whole_f32 * inv_rms[:, None] * whole_gain.astype(jnp.float32)[None, :]).astype(
            jnp.bfloat16
        )
        outgoing = jnp.einsum(
            "ect,td->ecd", place_bf, normed, preferred_element_type=jnp.float32
        ).astype(jnp.bfloat16)
        incoming = lax.all_to_all(outgoing, "expert", split_axis=0, concat_axis=0, tiled=True)
        inputs = incoming.reshape(experts * tok_rows, full_width)
        gate_rows, up_rows, down_rows = side_by_side(
            (w_gate[layer_idx, 0], w_up[layer_idx, 0], w_down[layer_idx, 0]), "dp", 0, 1
        )
        gate_val = lax.dot_general(inputs, gate_rows, contract, preferred_element_type=jnp.float32)
        up_val = lax.dot_general(inputs, up_rows, contract, preferred_element_type=jnp.float32)
        hidden = (jax.nn.silu(gate_val) * up_val).astype(jnp.bfloat16)
        partial_value = jnp.dot(hidden, down_rows, preferred_element_type=jnp.float32)
        summed = lax.psum_scatter(
            partial_value.astype(jnp.bfloat16), "mp", scatter_dimension=1, tiled=True
        )
        returned = lax.all_to_all(
            summed.reshape(experts, tok_rows, slice_width),
            "expert",
            split_axis=0,
            concat_axis=0,
            tiled=True,
        )
        place_weight = place_mask.astype(jnp.float32) * weight_te.T[:, None, :]
        update = jnp.einsum("ect,ecd->td", place_weight, returned.astype(jnp.float32))
        current = (current_f32 + update).astype(jnp.bfloat16)
    return current


def solution(mesh):
    in_specs = (
        P(("groups", "expert", "dp"), "mp"),
        P(None, "mp"),
        P(None, ("groups", "expert", "dp"), None),
        P(None, ("groups", "expert", "dp"), None),
        P(("groups", "expert", "dp")),
        P(None, "expert", ("mp", "dp"), None),
        P(None, "expert", ("mp", "dp"), None),
        P(None, "expert", ("mp", "dp"), None),
    )
    out_specs = P(("groups", "expert", "dp"), "mp")
    return jax.shard_map(body, mesh=mesh, in_specs=in_specs, out_specs=out_specs, check_vma=False)
```

profile of v0, /device:TPU:40, one launch (start us, length us, event | category | flops | bytes accessed | tf_op | source)
XLA Modules:
  0.0 336.3 jit_solution(16841984590572916138)
XLA Ops:
  6.5 0.0 all-gather.3.cloned.1.call-start
  6.6 0.0 copy-start
  6.6 0.0 copy-start.1
  6.6 2.5 slice_bitcast_fusion.5
  9.1 0.6 copy-done
  9.7 1.1 copy-done.1
  10.8 2.8 slice_bitcast_fusion.3
  13.6 5.6 %pad_maximum_fusion = bf16[224,12288]{1,0:T(8,128)(2,1)} fusion(bf16[224,4096]{1,0:T(8,128)(2,1)S(1)} %get-tuple-element.11, bf16[224,4096]{1,0:T(8,128)(2,1)S(1)} %get-tuple-element.22, bf16[224,4096]{1,0:T(8,128)(2,1)S(1)} %get-tuple-element.7), kind=kLoop, calls=%fused_computation | loop fusion | flops 16515072 | bytes 11010048 | tf_op jit(solution)/shard_map/concatenate | solution.py:26
  19.1 0.0 copy-start.6
  19.1 0.0 copy-start.5
  19.1 0.0 copy-start.4
  19.1 0.0 copy-start.2
  19.1 0.1 all-gather.3.cloned.1.call-update
  19.2 0.1 reduce-scatter.3.cloned.1.call-start
  19.3 0.5 copy-done.6
  19.8 0.0 copy-done.5
  19.8 0.1 copy.19
  19.9 0.1 reduce_window_sum.17
  20.0 0.1 copy.21
  20.1 0.0 copy-done.4
  20.1 0.0 copy-done.2
  20.2 51.8 %all_gather.12 = bf16[4096,65]{0,1:T(8,128)(2,1)S(1)} all-gather(bf16[256,65]{0,1:T(8,128)(2,1)S(1)} %pad_maximum_fusion.2), channel_id=1, replica_groups=mesh['groups'=2,'mp'=16,'expert'=4,'dp'=2] {'mp'}, dimensions={0}, use_global_device_ids=true | all-gather | bytes 565760 | tf_op jit(solution)/shard_map/all_gather | solution.py:13
  72.0 0.2 fusion.30
  72.2 0.9 convolution_convert_fusion.3
  73.1 23.9 %all_to_all.20 = bf16[4,64,4096]{2,1,0:T(8,128)(2,1)} all-to-all(bf16[4,64,4096]{2,1,0:T(8,128)(2,1)S(1)} %convolution_convert_fusion.3), channel_id=1, replica_groups=mesh['groups'=2,'mp'=16,'expert'=4,'dp'=2] {'expert'}, dimensions={0} | all-to-all | bytes 4194304 | tf_op jit(solution)/shard_map/all_to_all | solution.py:64
  97.0 0.0 all-gather.3.cloned.1.call-done
  97.0 3.8 %fusion.8 = f32[256,448]{0,1:T(8,128)S(1)} fusion(bf16[256,4096]{1,0:T(8,128)(2,1)} %bitcast.68, bf16[448,12288]{1,0:T(8,128)(2,1)} %all-gather.3.cloned.1.call-done), kind=kOutput, calls=%fused_computation.14 | convolution fusion | flops 939524096 | bytes 6225920 | tf_op jit(solution)/shard_map/dot_general | solution.py:69
  100.8 9.4 %convolution_convert_fusion.2 = bf16[256,4096]{1,0:T(8,128)(2,1)} fusion(bf16[448,12288]{1,0:T(8,128)(2,1)} %all-gather.3.cloned.1.call-done, bf16[256,4096]{1,0:T(8,128)(2,1)} %bitcast.69, f32[256,448]{0,1:T(8,128)S(1)} %fusion.8), kind=kOutput, calls=%fused_computation.4 | convolution fusion | flops 1880784896 | bytes 11993088 | tf_op jit(solution)/shard_map/dot_general | solution.py:72
  110.2 0.1 reduce-scatter.3.cloned.1.call-update
  110.2 0.1 all-gather.5.cloned.1.call-start
  110.3 4.9 %pad_maximum_fusion.1 = bf16[224,12288]{1,0:T(8,128)(2,1)} fusion(bf16[224,4096]{1,0:T(8,128)(2,1)} %get-tuple-element.12, bf16[224,4096]{1,0:T(8,128)(2,1)} %get-tuple-element.21, bf16[224,4096]{1,0:T(8,128)(2,1)S(1)} %get-tuple-element.8), kind=kLoop, calls=%fused_computation.1 | loop fusion | flops 16515072 | bytes 11010048 | tf_op jit(solution)/shard_map/concatenate | solution.py:26
  115.2 0.0 copy-start.3
  115.2 0.1 all-gather.5.cloned.1.call-update
  115.3 0.1 copy.23
  115.4 0.1 reduce_window_sum.18
  115.5 0.1 copy.25
  115.6 0.3 copy-done.3
  115.9 57.0 %reduce-scatter.3.cloned.1.call-done = bf16[256,256]{1,0:T(8,128)(2,1)} async-done(((bf16[256,4096]{1,0:T(8,128)(2,1)}), bf16[256,256]{1,0:T(8,128)(2,1)}) %reduce-scatter.3.cloned.1.call-update) | async-done | bytes 131088 | tf_op jit(solution)/shard_map/reduce_scatter | solution.py:73
  172.9 4.3 %all-to-all-start.1 = ((bf16[4,64,256]{2,1,0:T(8,128)(2,1)}), bf16[4,64,256]{2,1,0:T(8,128)(2,1)S(1)}, u32[]{:S(2)}, u32[]{:S(2)}) async-start(bf16[4,64,256]{2,1,0:T(8,128)(2,1)} %bitcast.70), calls=%async_computation.2 | async-start | bytes 262144 | tf_op jit(solution)/shard_map/all_to_all | solution.py:76
  177.3 6.0 %all-to-all-done.1 = bf16[4,64,256]{2,1,0:T(8,128)(2,1)S(1)} async-done(((bf16[4,64,256]{2,1,0:T(8,128)(2,1)}), bf16[4,64,256]{2,1,0:T(8,128)(2,1)S(1)}, u32[]{:S(2)}, u32[]{:S(2)}) %all-to-all-start.1) | async-done | bytes 131104 | tf_op jit(solution)/shard_map/all_to_all | solution.py:76
  183.2 0.3 fusion.29
  183.5 30.7 %all_gather.14 = bf16[4096,65]{0,1:T(8,128)(2,1)S(1)} all-gather(bf16[256,65]{0,1:T(8,128)(2,1)S(1)} %pad_maximum_fusion.3), channel_id=1, replica_groups=mesh['groups'=2,'mp'=16,'expert'=4,'dp'=2] {'mp'}, dimensions={0}, use_global_device_ids=true | all-gather | bytes 565760 | tf_op jit(solution)/shard_map/all_gather | solution.py:13
  214.3 0.2 fusion.33
  214.5 2.2 convolution_convert_fusion.1
  216.7 3.7 %all-to-all-start.2 = ((bf16[4,64,4096]{2,1,0:T(8,128)(2,1)}), bf16[4,64,4096]{2,1,0:T(8,128)(2,1)S(1)}, u32[]{:S(2)}, u32[]{:S(2)}) async-start(bf16[4,64,4096]{2,1,0:T(8,128)(2,1)} %convolution_convert_fusion.1), calls=%async_computation.3 | async-start | bytes 4194304 | tf_op jit(solution)/shard_map/all_to_all | solution.py:64
  220.4 0.2 reduce-scatter.5.cloned.1.call-start
  220.7 0.0 all-gather.5.cloned.1.call-done
  220.7 16.1 %all-to-all-done.2 = bf16[4,64,4096]{2,1,0:T(8,128)(2,1)S(1)} async-done(((bf16[4,64,4096]{2,1,0:T(8,128)(2,1)}), bf16[4,64,4096]{2,1,0:T(8,128)(2,1)S(1)}, u32[]{:S(2)}, u32[]{:S(2)}) %all-to-all-start.2) | async-done | bytes 2097184 | tf_op jit(solution)/shard_map/all_to_all | solution.py:64
  236.8 3.2 fusion.3
  240.0 8.8 %convolution_convert_fusion = bf16[256,4096]{1,0:T(8,128)(2,1)} fusion(bf16[448,12288]{1,0:T(8,128)(2,1)} %all-gather.5.cloned.1.call-done, bf16[256,4096]{1,0:T(8,128)(2,1)S(1)} %bitcast.67, f32[256,448]{0,1:T(8,128)S(1)} %fusion.3), kind=kOutput, calls=%fused_computation.2 | convolution fusion | flops 1880784896 | bytes 11993088 | tf_op jit(solution)/shard_map/dot_general | solution.py:72
  248.8 0.1 reduce-scatter.5.cloned.1.call-update
  248.9 69.8 %reduce-scatter.5.cloned.1.call-done = bf16[256,256]{1,0:T(8,128)(2,1)} async-done(((bf16[256,4096]{1,0:T(8,128)(2,1)}), bf16[256,256]{1,0:T(8,128)(2,1)}) %reduce-scatter.5.cloned.1.call-update) | async-done | bytes 131088 | tf_op jit(solution)/shard_map/reduce_scatter | solution.py:73
  318.7 4.2 %all-to-all-start.3 = ((bf16[4,64,256]{2,1,0:T(8,128)(2,1)}), bf16[4,64,256]{2,1,0:T(8,128)(2,1)S(1)}, u32[]{:S(2)}, u32[]{:S(2)}) async-start(bf16[4,64,256]{2,1,0:T(8,128)(2,1)} %bitcast.71), calls=%async_computation.5 | async-start | bytes 262144 | tf_op jit(solution)/shard_map/all_to_all | solution.py:76
  322.9 6.0 %all-to-all-done.3 = bf16[4,64,256]{2,1,0:T(8,128)(2,1)S(1)} async-done(((bf16[4,64,256]{2,1,0:T(8,128)(2,1)}), bf16[4,64,256]{2,1,0:T(8,128)(2,1)S(1)}, u32[]{:S(2)}, u32[]{:S(2)}) %all-to-all-start.3) | async-done | bytes 131104 | tf_op jit(solution)/shard_map/all_to_all | solution.py:76
  328.9 0.9 fusion.28
  (19 shorter events, 0.2 us)
Async XLA Ops:
  6.5 90.4 %all-gather.3.cloned.1.call-start = ((), (), s32[]{:S(2)}) async-start(), calls=%async_computation.6 | async-start | bytes 16515072 | tf_op jit(solution)/shard_map/all_gather | solution.py:27
  6.6 3.1 copy-start
  6.6 4.3 %copy-start.1 = (bf16[2,1,224,4096]{3,2,1,0:T(8,128)(2,1)S(1)}, bf16[2,1,224,4096]{3,2,1,0:T(8,128)(2,1)}, u32[]{:S(2)}) copy-start(bf16[2,1,224,4096]{3,2,1,0:T(8,128)(2,1)} %param.14) | copy-start | bytes 11010052
  19.1 0.7 copy-start.6
  19.1 0.7 copy-start.5
  19.1 1.0 copy-start.4
  19.1 1.0 copy-start.2
  19.2 153.7 %reduce-scatter.3.cloned.1.call-start = ((), (), s32[]{:S(2)}) async-start(), calls=%async_computation.7 | async-start | bytes 2228224 | tf_op jit(solution)/shard_map/reduce_scatter | solution.py:73
  110.2 110.5 %all-gather.5.cloned.1.call-start = ((), (), s32[]{:S(2)}) async-start(), calls=%async_computation.8 | async-start | bytes 16515072 | tf_op jit(solution)/shard_map/all_gather | solution.py:27
  115.2 0.7 copy-start.3
  172.9 10.3 %all-to-all-start.1 = ((bf16[4,64,256]{2,1,0:T(8,128)(2,1)}), bf16[4,64,256]{2,1,0:T(8,128)(2,1)S(1)}, u32[]{:S(2)}, u32[]{:S(2)}) async-start(bf16[4,64,256]{2,1,0:T(8,128)(2,1)} %bitcast.70), calls=%async_computation.2 | async-start | bytes 262144 | tf_op jit(solution)/shard_map/all_to_all | solution.py:76
  216.7 20.1 %all-to-all-start.2 = ((bf16[4,64,4096]{2,1,0:T(8,128)(2,1)}), bf16[4,64,4096]{2,1,0:T(8,128)(2,1)S(1)}, u32[]{:S(2)}, u32[]{:S(2)}) async-start(bf16[4,64,4096]{2,1,0:T(8,128)(2,1)} %convolution_convert_fusion.1), calls=%async_computation.3 | async-start | bytes 4194304 | tf_op jit(solution)/shard_map/all_to_all | solution.py:64
  220.4 98.3 %reduce-scatter.5.cloned.1.call-start = ((), (), s32[]{:S(2)}) async-start(), calls=%async_computation.9 | async-start | bytes 2228224 | tf_op jit(solution)/shard_map/reduce_scatter | solution.py:73
  318.7 10.2 %all-to-all-start.3 = ((bf16[4,64,256]{2,1,0:T(8,128)(2,1)}), bf16[4,64,256]{2,1,0:T(8,128)(2,1)S(1)}, u32[]{:S(2)}, u32[]{:S(2)}) async-start(bf16[4,64,256]{2,1,0:T(8,128)(2,1)} %bitcast.71), calls=%async_computation.5 | async-start | bytes 262144 | tf_op jit(solution)/shard_map/all_to_all | solution.py:76
Sparse Core Ops, SparseCore 0:
  19.3 45.2 all-gather.2
  110.4 62.5 reduce-scatter.2
  174.8 29.9 all-gather.4
  249.0 69.6 reduce-scatter.4
where the time goes:
time: 337 us; the launch traced here: 336 us
  waiting for transfers between devices  155 us (46%)
  blocking collectives  106 us (31%)
  matrix products  29.4 us (9%)
  between operations  13.3 us (4%)
  starting transfers between devices  12.6 us (4%)
  other arithmetic  11.3 us (3%)
  local copies, waits for them, and re-layouts  8.24 us (2%)
    reduce_scatter x2, waiting for transfers between devices, body(): lax.psum_scatter(partial_value.astype(jnp.bfloat16), 'mp', scatter_dimens...  127 us
    all_gather x2, blocking collectives, rows_first(): whole, at, outs = (lax.all_gather(both, axis, axis=0, tiled=True), 0, [])  82.5 us
    all_to_all x1, blocking collectives, body(): lax.all_to_all(outgoing, 'expert', split_axis=0, concat_axis=0, tiled=True)  23.9 us
    dot_general x2, matrix products, body(): jnp.dot(hidden, down_rows, preferred_element_type=jnp.float32)  18.2 us
    all_to_all x1, waiting for transfers between devices, body(): lax.all_to_all(outgoing, 'expert', split_axis=0, concat_axis=0, tiled=True)  16.1 us
    all_to_all x2, waiting for transfers between devices, body(): lax.all_to_all(summed.reshape(experts, tok_rows, slice_width), 'expert',...  11.9 us
    concatenate x2, other arithmetic, side_by_side(): both = jnp.concatenate(arrays, axis=along)  10.5 us
    all_to_all x2, starting transfers between devices, body(): lax.all_to_all(summed.reshape(experts, tok_rows, slice_width), 'expert',...  8.52 us
  transfers between devices with their start and end apart: 7, of which 5 were waited for; matrix products, arithmetic and copies ran while one was open for 3% of the time, Pallas kernels for 0%

commit v1 on v0

--- a/solution.py
+++ b/solution.py
@@ -5,6 +5,18 @@
 
 LAYERS = 2
 norm_floor = 0.1
+
+
+def cut_along(x, dim, size):
+    shape = x.shape
+    pieces = x.reshape(*shape[:dim], size, shape[dim] // size, *shape[dim + 1 :])
+    return jnp.moveaxis(pieces, dim, 0)
+
+
+def joined_along(tiles, dim):
+    dims = list(tiles.shape[1:])
+    dims[dim] *= tiles.shape[0]
+    return jnp.moveaxis(tiles, 0, dim).reshape(dims)
 
 
 def rows_first(arrays, axis, dims):
@@ -61,7 +73,14 @@
         outgoing = jnp.einsum(
             "ect,td->ecd", place_bf, normed, preferred_element_type=jnp.float32
         ).astype(jnp.bfloat16)
-        incoming = lax.all_to_all(outgoing, "expert", split_axis=0, concat_axis=0, tiled=True)
+        size, place = (lax.axis_size("expert"), lax.axis_index("expert"))
+        blocks = cut_along(outgoing, 0, size)
+        finished = [blocks[place]]
+        for turn in range(1, size):
+            sent = blocks[place ^ turn]
+            finished.append(lax.ppermute(sent, "expert", [(i, i ^ turn) for i in range(size)]))
+        blocks = jnp.stack(finished)[place ^ jnp.arange(size)]
+        incoming = joined_along(blocks, 0)
         inputs = incoming.reshape(experts * tok_rows, full_width)
         gate_rows, up_rows, down_rows = side_by_side(
             (w_gate[layer_idx, 0], w_up[layer_idx, 0], w_down[layer_idx, 0]), "dp", 0, 1

time: 337 us -> 339 us (level)
  blocking collectives: 106 us -> 82.3 us
  waiting for transfers between devices: 155 us -> 170 us
  local copies, waits for them, and re-layouts: 8.24 us -> 14.6 us
  starting transfers between devices: 12.6 us -> 18.4 us
    ppermute x0 -> x6, waiting for transfers between devices: none -> 32.6 us  [body(): lax.ppermute(sent, 'expert', [(i, i ^ turn) for i in range(size)])]
    all_to_all x1 -> x0, blocking collectives: 23.9 us -> none  [body(): lax.all_to_all(outgoing, 'expert', split_axis=0, concat_axis=0, tiled=True)]
    all_to_all x1 -> x0, waiting for transfers between devices: 16.1 us -> none  [body(): lax.all_to_all(outgoing, 'expert', split_axis=0, concat_axis=0, tiled=True)]
    ppermute x0 -> x6, starting transfers between devices: none -> 9.64 us  [body(): lax.ppermute(sent, 'expert', [(i, i ^ turn) for i in range(size)])]
    gather x0 -> x2, local copies, waits for them, and re-layouts: none -> 4.03 us  [body(): blocks = jnp.stack(finished)[place ^ jnp.arange(size)]]
    all_to_all x1 -> x0, starting transfers between devices: 3.7 us -> none  [body(): lax.all_to_all(outgoing, 'expert', split_axis=0, concat_axis=0, tiled=True)]
  transfers between devices with their start and end apart: 7 -> 12, of which waited for: 5 -> 10; matrix products, arithmetic and copies ran while one was open for 3% -> 4% of each run, Pallas kernels for 0% -> 0%
where the time goes in v1:
time: 339 us
  waiting for transfers between devices  170 us (50%)
  blocking collectives  82.3 us (24%)
  matrix products  28.4 us (8%)
  starting transfers between devices  18.4 us (5%)
  local copies, waits for them, and re-layouts  14.6 us (4%)
  between operations  13.3 us (4%)
  other arithmetic  11.8 us (3%)
    reduce_scatter x2, waiting for transfers between devices, body(): lax.psum_scatter(partial_value.astype(jnp.bfloat16), 'mp', scatter_dimens...  125 us
    all_gather x2, blocking collectives, rows_first(): whole, at, outs = (lax.all_gather(both, axis, axis=0, tiled=True), 0, [])  82.3 us
    ppermute x6, waiting for transfers between devices, body(): lax.ppermute(sent, 'expert', [(i, i ^ turn) for i in range(size)])  32.6 us
    dot_general x2, matrix products, body(): jnp.dot(hidden, down_rows, preferred_element_type=jnp.float32)  17.6 us
    all_to_all x2, waiting for transfers between devices, body(): lax.all_to_all(summed.reshape(experts, tok_rows, slice_width), 'expert',...  11.9 us
    concatenate x2, other arithmetic, side_by_side(): both = jnp.concatenate(arrays, axis=along)  10.5 us
    ppermute x6, starting transfers between devices, body(): lax.ppermute(sent, 'expert', [(i, i ^ turn) for i in range(size)])  9.64 us
    all_to_all x2, starting transfers between devices, body(): lax.all_to_all(summed.reshape(experts, tok_rows, slice_width), 'expert',...  8.47 us
  transfers between devices with their start and end apart: 12, of which 10 were waited for; matrix products, arithmetic and copies ran while one was open for 4% of the time, Pallas kernels for 0%

profile of v1, /device:TPU:40, one launch (start us, length us, event | category | flops | bytes accessed | tf_op | source)
XLA Modules:
  0.0 339.0 jit_solution(2961642594299645470)
XLA Ops:
  6.5 0.0 all-gather.3.cloned.1.call-start
  6.6 3.9 %slice_bitcast_fusion.5 = (bf16[224,4096]{1,0:T(8,128)(2,1)S(1)}, bf16[224,4096]{1,0:T(8,128)(2,1)}) fusion(bf16[2,1,224,4096]{3,2,1,0:T(8,128)(2,1)} %param.13), kind=kLoop, calls=%fused_computation.25 | loop fusion | bytes 7340032 | tf_op jit(solution)/shard_map/squeeze | solution.py:86
  10.4 0.0 copy-done.1
  10.4 1.0 copy-done.2
  11.5 2.7 slice_bitcast_fusion.3
  14.2 5.6 %pad_maximum_fusion = bf16[224,12288]{1,0:T(8,128)(2,1)} fusion(bf16[224,4096]{1,0:T(8,128)(2,1)S(1)} %get-tuple-element.11, bf16[224,4096]{1,0:T(8,128)(2,1)S(1)} %get-tuple-element.30, bf16[224,4096]{1,0:T(8,128)(2,1)S(1)} %get-tuple-element.7), kind=kLoop, calls=%fused_computation.2 | loop fusion | flops 16515072 | bytes 11010048 | tf_op jit(solution)/shard_map/concatenate | solution.py:38
  19.8 0.1 all-gather.3.cloned.1.call-update
  19.9 0.1 reduce-scatter.3.cloned.1.call-start
  19.9 0.5 copy-done.9
  20.4 0.0 copy-done.8
  20.5 0.1 copy.19
  20.6 0.1 reduce_window_sum.17
  20.7 0.1 copy.21
  20.8 0.0 copy-done.7
  20.8 0.0 copy-done.5
  20.8 51.8 %all_gather.12 = bf16[4096,65]{0,1:T(8,128)(2,1)S(1)} all-gather(bf16[256,65]{0,1:T(8,128)(2,1)S(1)} %pad_maximum_fusion.2), channel_id=1, replica_groups=mesh['groups'=2,'mp'=16,'expert'=4,'dp'=2] {'mp'}, dimensions={0}, use_global_device_ids=true | all-gather | bytes 565760 | tf_op jit(solution)/shard_map/all_gather | solution.py:25
  72.6 0.2 fusion.30
  72.9 0.9 convolution_convert_fusion.3
  73.7 0.2 dynamic-slice_bitcast_fusion.1
  74.0 1.7 collective-permute-start
  75.7 3.0 collective-permute-start.1
  78.7 0.1 collective-permute-start.2
  78.8 7.7 %collective-permute-done = bf16[1,64,4096]{2,1,0:T(8,128)(2,1)S(1)} collective-permute-done((bf16[1,64,4096]{2,1,0:T(8,128)(2,1)S(1)}, bf16[1,64,4096]{2,1,0:T(8,128)(2,1)S(1)}, u32[]{:S(2)}, u32[]{:S(2)}) %collective-permute-start) | collective-permute-done | bytes 524320 | tf_op jit(solution)/shard_map/ppermute | solution.py:81
  86.5 8.3 %collective-permute-done.1 = bf16[1,64,4096]{2,1,0:T(8,128)(2,1)S(1)} collective-permute-done((bf16[1,64,4096]{2,1,0:T(8,128)(2,1)S(1)}, bf16[1,64,4096]{2,1,0:T(8,128)(2,1)S(1)}, u32[]{:S(2)}, u32[]{:S(2)}) %collective-permute-start.1) | collective-permute-done | bytes 524320 | tf_op jit(solution)/shard_map/ppermute | solution.py:81
  94.8 2.5 collective-permute-done.2
  97.3 0.3 maximum_bitcast_fusion
  97.6 2.0 gather_fusion
  99.6 4.0 %fusion.8 = f32[256,448]{0,1:T(8,128)S(1)} fusion(bf16[256,4096]{1,0:T(8,128)(2,1)} %bitcast.84, bf16[448,12288]{1,0:T(8,128)(2,1)} %all-gather.3.cloned.1.call-done), kind=kOutput, calls=%fused_computation.16 | convolution fusion | flops 939524096 | bytes 6225920 | tf_op jit(solution)/shard_map/dot_general | solution.py:88
  103.6 0.0 copy-done.4
  103.6 8.8 %convolution_convert_fusion.2 = bf16[256,4096]{1,0:T(8,128)(2,1)} fusion(bf16[448,12288]{1,0:T(8,128)(2,1)} %all-gather.3.cloned.1.call-done, bf16[256,4096]{1,0:T(8,128)(2,1)S(1)} %bitcast.85, f32[256,448]{0,1:T(8,128)S(1)} %fusion.8), kind=kOutput, calls=%fused_computation.6 | convolution fusion | flops 1880784896 | bytes 11993088 | tf_op jit(solution)/shard_map/dot_general | solution.py:91
  112.4 0.1 reduce-scatter.3.cloned.1.call-update
  112.4 0.2 all-gather.5.cloned.1.call-start
  112.7 1.2 copy-done
  113.9 4.9 %pad_maximum_fusion.1 = bf16[224,12288]{1,0:T(8,128)(2,1)} fusion(bf16[224,4096]{1,0:T(8,128)(2,1)} %get-tuple-element.12, bf16[224,4096]{1,0:T(8,128)(2,1)} %get-tuple-element.29, bf16[224,4096]{1,0:T(8,128)(2,1)S(1)} %copy-done), kind=kLoop, calls=%fused_computation.3 | loop fusion | flops 16515072 | bytes 11010048 | tf_op jit(solution)/shard_map/concatenate | solution.py:38
  118.8 0.1 all-gather.5.cloned.1.call-update
  118.9 0.1 copy.23
  119.0 0.1 reduce_window_sum.18
  119.1 0.1 copy.25
  119.2 0.3 copy-done.6
  119.5 55.1 %reduce-scatter.3.cloned.1.call-done = bf16[256,256]{1,0:T(8,128)(2,1)} async-done(((bf16[256,4096]{1,0:T(8,128)(2,1)}), bf16[256,256]{1,0:T(8,128)(2,1)}) %reduce-scatter.3.cloned.1.call-update) | async-done | bytes 131088 | tf_op jit(solution)/shard_map/reduce_scatter | solution.py:92
  174.6 4.3 %all-to-all-start = ((bf16[4,64,256]{2,1,0:T(8,128)(2,1)}), bf16[4,64,256]{2,1,0:T(8,128)(2,1)S(1)}, u32[]{:S(2)}, u32[]{:S(2)}) async-start(bf16[4,64,256]{2,1,0:T(8,128)(2,1)} %bitcast.92), calls=%async_computation.1 | async-start | bytes 262144 | tf_op jit(solution)/shard_map/all_to_all | solution.py:95
  178.9 0.0 reduce-scatter.5.cloned.1.call-start
  178.9 6.0 %all-to-all-done = bf16[4,64,256]{2,1,0:T(8,128)(2,1)S(1)} async-done(((bf16[4,64,256]{2,1,0:T(8,128)(2,1)}), bf16[4,64,256]{2,1,0:T(8,128)(2,1)S(1)}, u32[]{:S(2)}, u32[]{:S(2)}) %all-to-all-start) | async-done | bytes 131104 | tf_op jit(solution)/shard_map/all_to_all | solution.py:95
  184.9 0.3 fusion.29
  185.2 30.5 %all_gather.14 = bf16[4096,65]{0,1:T(8,128)(2,1)S(1)} all-gather(bf16[256,65]{0,1:T(8,128)(2,1)S(1)} %pad_maximum_fusion.3), channel_id=1, replica_groups=mesh['groups'=2,'mp'=16,'expert'=4,'dp'=2] {'mp'}, dimensions={0}, use_global_device_ids=true | all-gather | bytes 565760 | tf_op jit(solution)/shard_map/all_gather | solution.py:25
  215.7 0.2 fusion.33
  215.9 0.9 convolution_convert_fusion.1
  216.8 0.2 dynamic-slice_bitcast_fusion
  217.0 0.7 collective-permute-start.3
  217.7 2.1 collective-permute-start.4
  219.9 2.0 collective-permute-start.5
  221.8 4.5 %collective-permute-done.3 = bf16[1,64,4096]{2,1,0:T(8,128)(2,1)S(1)} collective-permute-done((bf16[1,64,4096]{2,1,0:T(8,128)(2,1)S(1)}, bf16[1,64,4096]{2,1,0:T(8,128)(2,1)S(1)}, u32[]{:S(2)}, u32[]{:S(2)}) %collective-permute-start.3) | collective-permute-done | bytes 524320 | tf_op jit(solution)/shard_map/ppermute | solution.py:81
  226.3 6.4 %collective-permute-done.4 = bf16[1,64,4096]{2,1,0:T(8,128)(2,1)S(1)} collective-permute-done((bf16[1,64,4096]{2,1,0:T(8,128)(2,1)S(1)}, bf16[1,64,4096]{2,1,0:T(8,128)(2,1)S(1)}, u32[]{:S(2)}, u32[]{:S(2)}) %collective-permute-start.4) | collective-permute-done | bytes 524320 | tf_op jit(solution)/shard_map/ppermute | solution.py:81
  232.7 3.1 collective-permute-done.5
  235.9 0.3 maximum_bitcast_fusion.1
  236.1 2.0 gather_fusion.1
  238.2 4.0 %fusion.3 = f32[256,448]{0,1:T(8,128)S(1)} fusion(bf16[256,4096]{1,0:T(8,128)(2,1)} %bitcast.82, bf16[448,12288]{1,0:T(8,128)(2,1)} %all-gather.5.cloned.1.call-done), kind=kOutput, calls=%fused_computation.11 | convolution fusion | flops 939524096 | bytes 6225920 | tf_op jit(solution)/shard_map/dot_general | solution.py:88
  242.1 0.0 copy-done.3
  242.1 8.8 %convolution_convert_fusion = bf16[256,4096]{1,0:T(8,128)(2,1)} fusion(bf16[448,12288]{1,0:T(8,128)(2,1)} %all-gather.5.cloned.1.call-done, bf16[256,4096]{1,0:T(8,128)(2,1)S(1)} %bitcast.83, f32[256,448]{0,1:T(8,128)S(1)} %fusion.3), kind=kOutput, calls=%fused_computation.4 | convolution fusion | flops 1880784896 | bytes 11993088 | tf_op jit(solution)/shard_map/dot_general | solution.py:91
  250.9 0.1 reduce-scatter.5.cloned.1.call-update
  251.0 70.4 %reduce-scatter.5.cloned.1.call-done = bf16[256,256]{1,0:T(8,128)(2,1)} async-done(((bf16[256,4096]{1,0:T(8,128)(2,1)}), bf16[256,256]{1,0:T(8,128)(2,1)}) %reduce-scatter.5.cloned.1.call-update) | async-done | bytes 131088 | tf_op jit(solution)/shard_map/reduce_scatter | solution.py:92
  321.4 4.2 %all-to-all-start.1 = ((bf16[4,64,256]{2,1,0:T(8,128)(2,1)}), bf16[4,64,256]{2,1,0:T(8,128)(2,1)S(1)}, u32[]{:S(2)}, u32[]{:S(2)}) async-start(bf16[4,64,256]{2,1,0:T(8,128)(2,1)} %bitcast.93), calls=%async_computation.3 | async-start | bytes 262144 | tf_op jit(solution)/shard_map/all_to_all | solution.py:95
  325.5 6.0 %all-to-all-done.1 = bf16[4,64,256]{2,1,0:T(8,128)(2,1)S(1)} async-done(((bf16[4,64,256]{2,1,0:T(8,128)(2,1)}), bf16[4,64,256]{2,1,0:T(8,128)(2,1)S(1)}, u32[]{:S(2)}, u32[]{:S(2)}) %all-to-all-start.1) | async-done | bytes 131104 | tf_op jit(solution)/shard_map/all_to_all | solution.py:95
  331.5 0.9 fusion.28
  (33 shorter events, 0.2 us)
Async XLA Ops:
  6.5 93.1 %all-gather.3.cloned.1.call-start = ((), (), s32[]{:S(2)}) async-start(), calls=%async_computation.4 | async-start | bytes 16515072 | tf_op jit(solution)/shard_map/all_gather | solution.py:39
  6.6 3.9 %copy-start.1 = (bf16[2,1,224,4096]{3,2,1,0:T(8,128)(2,1)S(1)}, bf16[2,1,224,4096]{3,2,1,0:T(8,128)(2,1)}, u32[]{:S(2)}) copy-start(bf16[2,1,224,4096]{3,2,1,0:T(8,128)(2,1)} %param.15) | copy-start | bytes 11010052
  6.6 4.9 %copy-start.2 = (bf16[2,1,224,4096]{3,2,1,0:T(8,128)(2,1)S(1)}, bf16[2,1,224,4096]{3,2,1,0:T(8,128)(2,1)}, u32[]{:S(2)}) copy-start(bf16[2,1,224,4096]{3,2,1,0:T(8,128)(2,1)} %param.14) | copy-start | bytes 11010052
  19.8 0.7 copy-start.9
  19.8 0.7 copy-start.8
  19.8 1.0 copy-start.7
  19.8 1.0 copy-start.5
  19.9 154.7 %reduce-scatter.3.cloned.1.call-start = ((), (), s32[]{:S(2)}) async-start(), calls=%async_computation.5 | async-start | bytes 2228224 | tf_op jit(solution)/shard_map/reduce_scatter | solution.py:92
  74.0 12.5 %collective-permute-start = (bf16[1,64,4096]{2,1,0:T(8,128)(2,1)S(1)}, bf16[1,64,4096]{2,1,0:T(8,128)(2,1)S(1)}, u32[]{:S(2)}, u32[]{:S(2)}) collective-permute-start(bf16[1,64,4096]{2,1,0:T(8,128)(2,1)S(1)} %get-tuple-element.20), channel_id=1, source_target_pairs={{0,2},{2,0},{4,6},{6,4},{1,3},{3,1},{5,7},{7,5},{8,10},{10,8},{12,... | collective-permute-start | bytes 1572872 | tf_op jit(solution)/shard_map/ppermute | solution.py:81
  75.7 19.1 %collective-permute-start.1 = (bf16[1,64,4096]{2,1,0:T(8,128)(2,1)S(1)}, bf16[1,64,4096]{2,1,0:T(8,128)(2,1)S(1)}, u32[]{:S(2)}, u32[]{:S(2)}) collective-permute-start(bf16[1,64,4096]{2,1,0:T(8,128)(2,1)S(1)} %get-tuple-element.19), channel_id=1, source_target_pairs={{0,4},{2,6},{4,0},{6,2},{1,5},{3,7},{5,1},{7,3},{8,12},{10,14},{12... | collective-permute-start | bytes 1572872 | tf_op jit(solution)/shard_map/ppermute | solution.py:81
  78.7 18.6 %collective-permute-start.2 = (bf16[1,64,4096]{2,1,0:T(8,128)(2,1)S(1)}, bf16[1,64,4096]{2,1,0:T(8,128)(2,1)S(1)}, u32[]{:S(2)}, u32[]{:S(2)}) collective-permute-start(bf16[1,64,4096]{2,1,0:T(8,128)(2,1)S(1)} %get-tuple-element.18), channel_id=1, source_target_pairs={{0,6},{2,4},{4,2},{6,0},{1,7},{3,5},{5,3},{7,1},{8,14},{10,12},{12... | collective-permute-start | bytes 1572872 | tf_op jit(solution)/shard_map/ppermute | solution.py:81
  99.6 4.0 %copy-start.4 = (bf16[4,64,4096]{2,1,0:T(8,128)(2,1)S(1)}, bf16[4,64,4096]{2,1,0:T(8,128)(2,1)}, u32[]{:S(2)}) copy-start(bf16[4,64,4096]{2,1,0:T(8,128)(2,1)} %gather_fusion) | copy-start | bytes 6291460
  112.4 1.5 copy-start
  112.4 125.7 %all-gather.5.cloned.1.call-start = ((), (), s32[]{:S(2)}) async-start(), calls=%async_computation.6 | async-start | bytes 16515072 | tf_op jit(solution)/shard_map/all_gather | solution.py:39
  118.8 0.7 copy-start.6
  174.6 10.3 %all-to-all-start = ((bf16[4,64,256]{2,1,0:T(8,128)(2,1)}), bf16[4,64,256]{2,1,0:T(8,128)(2,1)S(1)}, u32[]{:S(2)}, u32[]{:S(2)}) async-start(bf16[4,64,256]{2,1,0:T(8,128)(2,1)} %bitcast.92), calls=%async_computation.1 | async-start | bytes 262144 | tf_op jit(solution)/shard_map/all_to_all | solution.py:95
  178.9 142.5 %reduce-scatter.5.cloned.1.call-start = ((), (), s32[]{:S(2)}) async-start(), calls=%async_computation.7 | async-start | bytes 2228224 | tf_op jit(solution)/shard_map/reduce_scatter | solution.py:92
  217.0 9.3 %collective-permute-start.3 = (bf16[1,64,4096]{2,1,0:T(8,128)(2,1)S(1)}, bf16[1,64,4096]{2,1,0:T(8,128)(2,1)S(1)}, u32[]{:S(2)}, u32[]{:S(2)}) collective-permute-start(bf16[1,64,4096]{2,1,0:T(8,128)(2,1)S(1)} %get-tuple-element.16), channel_id=1, source_target_pairs={{0,2},{2,0},{4,6},{6,4},{1,3},{3,1},{5,7},{7,5},{8,10},{10,8},{12,... | collective-permute-start | bytes 1572872 | tf_op jit(solution)/shard_map/ppermute | solution.py:81
  217.7 15.0 %collective-permute-start.4 = (bf16[1,64,4096]{2,1,0:T(8,128)(2,1)S(1)}, bf16[1,64,4096]{2,1,0:T(8,128)(2,1)S(1)}, u32[]{:S(2)}, u32[]{:S(2)}) collective-permute-start(bf16[1,64,4096]{2,1,0:T(8,128)(2,1)S(1)} %get-tuple-element.15), channel_id=1, source_target_pairs={{0,4},{2,6},{4,0},{6,2},{1,5},{3,7},{5,1},{7,3},{8,12},{10,14},{12... | collective-permute-start | bytes 1572872 | tf_op jit(solution)/shard_map/ppermute | solution.py:81
  219.9 16.0 %collective-permute-start.5 = (bf16[1,64,4096]{2,1,0:T(8,128)(2,1)S(1)}, bf16[1,64,4096]{2,1,0:T(8,128)(2,1)S(1)}, u32[]{:S(2)}, u32[]{:S(2)}) collective-permute-start(bf16[1,64,4096]{2,1,0:T(8,128)(2,1)S(1)} %get-tuple-element.14), channel_id=1, source_target_pairs={{0,6},{2,4},{4,2},{6,0},{1,7},{3,5},{5,3},{7,1},{8,14},{10,12},{12... | collective-permute-start | bytes 1572872 | tf_op jit(solution)/shard_map/ppermute | solution.py:81
  238.2 4.0 %copy-start.3 = (bf16[4,64,4096]{2,1,0:T(8,128)(2,1)S(1)}, bf16[4,64,4096]{2,1,0:T(8,128)(2,1)}, u32[]{:S(2)}) copy-start(bf16[4,64,4096]{2,1,0:T(8,128)(2,1)} %gather_fusion.1) | copy-start | bytes 6291460
  321.4 10.1 %all-to-all-start.1 = ((bf16[4,64,256]{2,1,0:T(8,128)(2,1)}), bf16[4,64,256]{2,1,0:T(8,128)(2,1)S(1)}, u32[]{:S(2)}, u32[]{:S(2)}) async-start(bf16[4,64,256]{2,1,0:T(8,128)(2,1)} %bitcast.93), calls=%async_computation.3 | async-start | bytes 262144 | tf_op jit(solution)/shard_map/all_to_all | solution.py:95
Sparse Core Ops, SparseCore 0:
  20.0 45.2 all-gather.2
  112.6 61.9 reduce-scatter.2
  176.4 29.7 all-gather.4
  251.1 70.2 reduce-scatter.4
